TPU v7x, 128 devices: a whole 4x4x4 slice. The times are simulated.
128 devices in a mesh: cp: 32 (over x, y, core), tp: 4 (over z).
Axes of the slice: x: 4, y: 4, z: 4, core: 2. Of those that a mesh axis runs over, the one named last changes fastest.
Arguments:
- hidden: bfloat16 [8192, 4096], P('cp', 'tp'), may hold values from -120 to 120
- query_weight: bfloat16 [4096, 4096], P(None, 'tp'), may hold values from -0.1875 to 0.1875
- key_matrix: bfloat16 [4096, 512], P(None, 'tp'), may hold values from -0.09375 to 0.09375
- value_matrix: bfloat16 [4096, 512], P(None, 'tp'), may hold values from -0.09375 to 0.09375
- output_weight: bfloat16 [4096, 4096], P('tp'), may hold values from -0.1875 to 0.1875
- document_bounds: int32 [9], replicated, may hold values from 0 to 8192, as said below
- block_owner: int32 [64], replicated, may hold values from 0 to 31, as said below
Outputs:
- attended: bfloat16 [8192, 4096], P('cp', 'tp')
Inputs may be any that keep to these rules, and one draw needn't show every extreme that they name: document_bounds[0] = 0, document_bounds[8] = 8192, strictly rising; document i holds the tokens from document_bounds[i] to document_bounds[i + 1] - 1. `block_owner`: every index of cp is named by exactly 2 blocks.
All inputs are finite; a program needn't handle non-finite values.
Results may differ from a plain program's by a relative error of at most 0.012.
The roundings to bfloat16 on the way count: a program that leaves them out, or rounds other values in their place, can miss the bound.
Values may be sent and summed in bfloat16 or wider, within the bound.
A program may use at most 128 MiB of HBM per device.

v0:
```python
import math
import jax
import jax.numpy as jnp
from jax import lax
from jax.sharding import PartitionSpec as P

HEAD_WIDTH = 128
BLOCK = 128
rope_theta = 500000.0
rope_factor = 8.0
rope_context = 8192.0
masked_score = -1e30


def in_one_piece(arrays, axis, dim, along):
    both = jnp.concatenate(arrays, axis=along)
    filled, at, outs = (lax.all_gather(both, axis, axis=dim, tiled=True), 0, [])
    for a in arrays:
        outs.append(lax.slice_in_dim(filled, at, at + a.shape[along], axis=along))
        at += a.shape[along]
    return tuple(outs)


def rope_inverse(head_size):
    halves = jnp.arange(head_size // 2, dtype=jnp.float32)
    inverse = 1.0 / rope_theta ** (2.0 * halves / head_size)
    wavelength = 2.0 * math.pi / inverse
    smooth = (rope_context / wavelength - 1.0) / 3.0
    blended = (1.0 - smooth) * inverse / rope_factor + smooth * inverse
    longer = jnp.where(wavelength > rope_context, inverse / rope_factor, blended)
    return jnp.where(wavelength < rope_context / 4.0, inverse, longer)


def document_of(tokens, bounds):
    inner_bounds = bounds[1:-1]
    return jnp.sum((tokens[:, None] >= inner_bounds[None, :]).astype(jnp.int32), axis=1)


def position_of(tokens, bounds):
    starts = bounds[:-1]
    document_start = jnp.max(
        jnp.where(starts[None, :] <= tokens[:, None], starts[None, :], 0), axis=1
    )
    return tokens - document_start


def rotate(raw_rows, tokens, bounds, head_size):
    row_count = raw_rows.shape[0]
    head_count = raw_rows.shape[1] // head_size
    angles = (
        position_of(tokens, bounds).astype(jnp.float32)[:, None] * rope_inverse(head_size)[None, :]
    )
    cosine = jnp.cos(angles)[:, None, :]
    sine_table = jnp.sin(angles)[:, None, :]
    heads_view = raw_rows.reshape(row_count, head_count, head_size)
    front_half = heads_view[:, :, : head_size // 2]
    back_half = heads_view[:, :, head_size // 2 :]
    turned = jnp.concatenate(
        [
            front_half * cosine - back_half * sine_table,
            back_half * cosine + front_half * sine_table,
        ],
        axis=2,
    )
    return turned.reshape(row_count, head_count * head_size).astype(jnp.bfloat16)


def owner_order(block_owner, per_device):
    block_count = block_owner.shape[0]
    blocks = jnp.arange(block_count, dtype=jnp.int32)
    same_owner = block_owner[:, None] == block_owner[None, :]
    earlier = blocks[None, :] < blocks[:, None]
    owner_rank = jnp.sum((same_owner & earlier).astype(jnp.int32), axis=1)
    target = block_owner * per_device + owner_rank
    return jnp.sum(jnp.where(target[None, :] == blocks[:, None], blocks[None, :], 0), axis=1)


def relayout(local_rows, block_order):
    cp_size = lax.axis_size("cp")
    row_count, row_width = local_rows.shape
    per_device = row_count // BLOCK
    portion = BLOCK // cp_size
    pieces = local_rows.reshape(per_device, cp_size, portion * row_width)
    spread = lax.all_to_all(pieces, "cp", split_axis=1, concat_axis=0, tiled=True)
    spread = spread.reshape(per_device * cp_size, portion * row_width)
    wanted = block_order.reshape(cp_size, per_device).T.reshape(-1)
    outgoing = jnp.take(spread, wanted, axis=0).reshape(per_device, cp_size, portion * row_width)
    arrived = lax.all_to_all(outgoing, "cp", split_axis=1, concat_axis=1, tiled=True)
    return arrived.reshape(row_count, row_width)


def project(local_rows, query_weight, key_matrix, value_matrix):
    weight_list = (query_weight, key_matrix, value_matrix)
    portion = lax.all_gather(local_rows, "tp", axis=1, tiled=True)
    return tuple(
        (jnp.dot(portion, weight, preferred_element_type=jnp.float32) for weight in weight_list)
    )


def attend(queries, query_tokens, key_rows, value_rows, key_tokens, bounds, head_size, kv_heads):
    row_count = queries.shape[0]
    query_group_width = queries.shape[1] // (kv_heads * head_size)
    grouped = queries.reshape(row_count, kv_heads, query_group_width, head_size).transpose(
        1, 2, 0, 3
    )
    grouped = grouped.reshape(kv_heads, query_group_width * row_count, head_size)
    query_documents = document_of(query_tokens, bounds)
    score_scale = 1.0 / math.sqrt(head_size)

    def update(flash_state, key_block, value_block, token_block):
        block_rows = key_block.shape[0]
        key_documents = document_of(token_block, bounds)
        allowed = (query_documents[:, None] == key_documents[None, :]) & (
            token_block[None, :] <= query_tokens[:, None]
        )

        def compute(inner_state):
            running_max, running_sum, running_out = inner_state
            per_head_keys = key_block.reshape(block_rows, kv_heads, head_size).transpose(1, 0, 2)
            per_head_values = value_block.reshape(block_rows, kv_heads, head_size).transpose(
                1, 0, 2
            )
            scores = (
                jnp.einsum(
                    "khd,ksd->khs", grouped, per_head_keys, preferred_element_type=jnp.float32
                )
                * score_scale
            )
            wide_mask = jnp.tile(allowed, (query_group_width, 1))[None, :, :]
            scores = jnp.where(wide_mask, scores, masked_score)
            new_max = jnp.maximum(running_max, jnp.max(scores, axis=2))
            weights = jnp.where(wide_mask, jnp.exp(scores - new_max[:, :, None]), 0.0)
            factor = jnp.exp(running_max - new_max)
            new_sum = running_sum * factor + jnp.sum(weights, axis=2)
            new_out = running_out * factor[:, :, None] + jnp.einsum(
                "khs,ksd->khd",
                weights.astype(jnp.bfloat16),
                per_head_values,
                preferred_element_type=jnp.float32,
            )
            return (new_max, new_sum, new_out)

        return lax.cond(jnp.any(allowed), compute, lambda inner_state: inner_state, flash_state)

    initial = (
        jnp.full((kv_heads, query_group_width * row_count), masked_score, jnp.float32),
        jnp.zeros((kv_heads, query_group_width * row_count), jnp.float32),
        jnp.zeros((kv_heads, query_group_width * row_count, head_size), jnp.float32),
    )
    key_part, value_part, token_part = (
        *in_one_piece((key_rows, value_rows), "cp", 0, 1),
        lax.all_gather(key_tokens, "cp", axis=0, tiled=True),
    )
    part_rows = key_part.shape[0]
    block_rows = math.gcd(part_rows, 512)

    def one_block(block_index, inner_state):
        first_row = block_index * block_rows
        return update(
            inner_state,
            lax.dynamic_slice_in_dim(key_part, first_row, block_rows, 0),
            lax.dynamic_slice_in_dim(value_part, first_row, block_rows, 0),
            lax.dynamic_slice_in_dim(token_part, first_row, block_rows, 0),
        )

    final_max, final_sum, final_out = lax.fori_loop(0, part_rows // block_rows, one_block, initial)
    normalized = final_out / final_sum[:, :, None]
    merged = normalized.reshape(kv_heads, query_group_width, row_count, head_size).transpose(
        2, 0, 1, 3
    )
    return merged.reshape(row_count, kv_heads * query_group_width * head_size).astype(jnp.bfloat16)


def output_rows(heads_out, output_weight):
    head_terms = jnp.dot(heads_out, output_weight, preferred_element_type=jnp.float32)
    return lax.psum_scatter(head_terms.astype(jnp.bfloat16), "tp", scatter_dimension=1, tiled=True)


def local(
    hidden, query_weight, key_matrix, value_matrix, output_weight, document_bounds, block_owner
):
    cp_index = lax.axis_index("cp")
    row_count = hidden.shape[0]
    per_device = row_count // BLOCK
    block_order = owner_order(block_owner, per_device)
    own_blocks = lax.dynamic_slice_in_dim(block_order, cp_index * per_device, per_device, 0)
    new_tokens = (
        own_blocks[:, None] * BLOCK + jnp.arange(BLOCK, dtype=jnp.int32)[None, :]
    ).reshape(-1)
    kv_heads = key_matrix.shape[1] // HEAD_WIDTH
    query_raw, key_raw, value_raw = project(hidden, query_weight, key_matrix, value_matrix)
    key_tokens = cp_index * row_count + jnp.arange(row_count, dtype=jnp.int32)
    queries = relayout(rotate(query_raw, key_tokens, document_bounds, HEAD_WIDTH), block_order)
    key_rows = rotate(key_raw, key_tokens, document_bounds, HEAD_WIDTH)
    value_rows = value_raw.astype(jnp.bfloat16)
    heads_out = attend(
        queries, new_tokens, key_rows, value_rows, key_tokens, document_bounds, HEAD_WIDTH, kv_heads
    )
    return output_rows(heads_out, output_weight)


def solution(mesh):
    placed = (P("cp", "tp"), P(None, "tp"), P(None, "tp"), P(None, "tp"), P("tp", None), P(), P())
    return jax.shard_map(
        local, mesh=mesh, in_specs=placed, out_specs=P("cp", "tp"), check_vma=False
    )
```

profile of v0, /device:TPU:1, one launch (start us, length us, event | category | flops | bytes accessed | tf_op | source)
XLA Modules:
  0.0 271.1 jit_solution(13011074800097958751)
XLA Ops:
  6.5 0.7 all-gather.4.cloned.1.call-update
  7.3 0.7 select_reduce_fusion.1
  8.1 35.0 %all-gather.4.cloned.1.call-done = bf16[256,4096]{1,0:T(8,128)(2,1)} async-done(((bf16[256,1024]{1,0:T(8,128)(2,1)}), bf16[256,4096]{1,0:T(8,128)(2,1)}) %all-gather.4.cloned.1.call-update) | async-done | bytes 2097168 | tf_op jit(solution)/shard_map/all_gather | solution.py:94
  43.1 2.6 convolution_bitcast_fusion.2
  46.0 2.7 convolution_convert_fusion.1
  48.7 0.7 pad_maximum_fusion.1
  49.9 0.5 multiply_cosine_fusion
  50.5 5.7 %convolution_bitcast_fusion.1 = f32[32,8,8,128]{3,1,2,0:T(8,128)S(1)} fusion(bf16[256,4096]{1,0:T(8,128)(2,1)S(1)} %copy-done.1, bf16[4096,1024]{1,0:T(8,128)(2,1)} %param.12), kind=kOutput, calls=%fused_computation.28 | convolution fusion | flops 2147483648 | bytes 11534336 | tf_op jit(solution)/shard_map/dot_general | solution.py:96
  56.4 0.5 subtract_convert_fusion
  57.5 1.3 copy.48
  58.8 7.7 %all-to-all-start = ((bf16[2,32,4096]{2,0,1:T(2,128)(2,1)}), bf16[2,32,4096]{2,0,1:T(2,128)(2,1)S(1)}, u32[]{:S(2)}, u32[]{:S(2)}) async-start(bf16[2,32,4096]{2,0,1:T(2,128)(2,1)} %copy.48), calls=%async_computation | async-start | bytes 1048576 | tf_op jit(solution)/shard_map/all_to_all | solution.py:84
  66.6 11.5 %all-to-all-done = bf16[2,32,4096]{2,0,1:T(2,128)(2,1)S(1)} async-done(((bf16[2,32,4096]{2,0,1:T(2,128)(2,1)}), bf16[2,32,4096]{2,0,1:T(2,128)(2,1)S(1)}, u32[]{:S(2)}, u32[]{:S(2)}) %all-to-all-start) | async-done | bytes 524320 | tf_op jit(solution)/shard_map/all_to_all | solution.py:84
  78.3 0.9 gather_fusion
  79.2 1.5 broadcast_select_fusion
  80.7 4.0 %all-to-all-start.1 = ((bf16[2,32,4096]{2,0,1:T(2,128)(2,1)}), bf16[2,32,4096]{2,0,1:T(2,128)(2,1)S(1)}, u32[]{:S(2)}, u32[]{:S(2)}) async-start(bf16[2,32,4096]{2,0,1:T(2,128)(2,1)} %broadcast_select_fusion), calls=%async_computation.1 | async-start | bytes 1048576 | tf_op jit(solution)/shard_map/all_to_all | solution.py:88
  84.8 27.8 %all-gather = s32[32,1,256]{2,1,0:T(1,128)S(1)} all-gather(s32[1,1,256]{2,1,0:T(1,128)S(1)} %bitcast.88), channel_id=1, replica_groups=mesh['cp'=32,'tp'=4] {'cp'}, dimensions={0}, use_global_device_ids=true | all-gather | bytes 33792 | tf_op jit(solution)/shard_map/all_gather | solution.py:152
  113.4 0.9 copy.52
  114.2 3.9 %fusion.31 = (bf16[8192,128]{0,1:T(8,128)(2,1)}, bf16[8192,128]{0,1:T(8,128)(2,1)S(1)}) fusion(bf16[8192,256]{0,1:T(8,128)(2,1)} %all-gather.6.cloned.1.call-done), kind=kLoop, calls=%fused_computation.70 | loop fusion | bytes 8388608 | tf_op jit(solution)/shard_map/slice | solution.py:19
  118.1 4.1 %copy.54 = bf16[8192,128]{1,0:T(8,128)(2,1)} copy(bf16[8192,128]{0,1:T(8,128)(2,1)} %get-tuple-element.405) | data formatting | bytes 4194304
  122.2 2.4 copy.53
  124.8 63.4 %while.18 = (s32[]{:T(128)}, f32[1,2048]{1,0:T(1,128)S(1)}, f32[1,2048]{1,0:T(1,128)S(1)}, f32[1,2048,128]{2,1,0:T(8,128)S(1)}, s32[256]{0:T(256)S(1)}, /*index=...) while((s32[]{:T(128)}, f32[1,2048]{1,0:T(1,128)S(1)}, ...), condition=%wide.region_11.12_spmd.clone, body=%wide.region_4.11_spmd.clone.sunk | while | flops 551565568 | bytes 22167960 | solution.py:166
  125.1 0.8 fusion.41
  126.8 0.8 fusion.41
  128.6 0.8 fusion.41
  130.3 0.8 fusion.41
  132.1 0.8 fusion.41
  133.8 0.8 fusion.41
  135.6 0.8 fusion.41
  137.3 0.8 fusion.41
  138.7 7.1 %conditional.3 = ((f32[1,2048]{1,0:T(1,128)S(1)}, f32[1,2048]{1,0:T(1,128)S(1)}, f32[1,2048,128]{2,1,0:T(8,128)S(1)})) conditional(s32[]{:T(128)} %convert_element_type.86, (f32[1,2048]{1,0:T(1,128)S(1)}, f32[1,2048]{1,0:T(1,128)S(1)}, f32[1,2048,128]{2,1,0:T(8,128)S(1)}) %tuple.62, (pred[256,512]{0,1:T(8,128)(4,1)S(1)}, ...), branch_computations={%region_7.7_spmd, %region_8.10_spmd} | conditional | flops 551030784 | bytes 22021152 | solution.py:143
  139.2 0.6 copy.56
  139.8 2.0 fusion.2
  141.9 1.2 fusion.4
  143.1 2.7 fusion.5
  146.1 0.8 fusion.41
  147.5 7.1 %conditional.3 = ((f32[1,2048]{1,0:T(1,128)S(1)}, f32[1,2048]{1,0:T(1,128)S(1)}, f32[1,2048,128]{2,1,0:T(8,128)S(1)})) conditional(s32[]{:T(128)} %convert_element_type.86, (f32[1,2048]{1,0:T(1,128)S(1)}, f32[1,2048]{1,0:T(1,128)S(1)}, f32[1,2048,128]{2,1,0:T(8,128)S(1)}) %tuple.62, (pred[256,512]{0,1:T(8,128)(4,1)S(1)}, ...), branch_computations={%region_7.7_spmd, %region_8.10_spmd} | conditional | flops 551030784 | bytes 22021152 | solution.py:143
  148.0 0.6 copy.56
  148.7 2.0 fusion.2
  150.7 1.2 fusion.4
  152.0 2.7 fusion.5
  155.0 0.8 fusion.41
  156.4 7.1 %conditional.3 = ((f32[1,2048]{1,0:T(1,128)S(1)}, f32[1,2048]{1,0:T(1,128)S(1)}, f32[1,2048,128]{2,1,0:T(8,128)S(1)})) conditional(s32[]{:T(128)} %convert_element_type.86, (f32[1,2048]{1,0:T(1,128)S(1)}, f32[1,2048]{1,0:T(1,128)S(1)}, f32[1,2048,128]{2,1,0:T(8,128)S(1)}) %tuple.62, (pred[256,512]{0,1:T(8,128)(4,1)S(1)}, ...), branch_computations={%region_7.7_spmd, %region_8.10_spmd} | conditional | flops 551030784 | bytes 22021152 | solution.py:143
  156.9 0.6 copy.56
  157.5 2.0 fusion.2
  159.5 1.2 fusion.4
  160.8 2.7 fusion.5
  163.8 0.8 fusion.41
  165.6 0.8 fusion.41
  167.3 0.8 fusion.41
  169.1 0.8 fusion.41
  170.5 7.1 %conditional.3 = ((f32[1,2048]{1,0:T(1,128)S(1)}, f32[1,2048]{1,0:T(1,128)S(1)}, f32[1,2048,128]{2,1,0:T(8,128)S(1)})) conditional(s32[]{:T(128)} %convert_element_type.86, (f32[1,2048]{1,0:T(1,128)S(1)}, f32[1,2048]{1,0:T(1,128)S(1)}, f32[1,2048,128]{2,1,0:T(8,128)S(1)}) %tuple.62, (pred[256,512]{0,1:T(8,128)(4,1)S(1)}, ...), branch_computations={%region_7.7_spmd, %region_8.10_spmd} | conditional | flops 551030784 | bytes 22021152 | solution.py:143
  171.0 0.6 copy.56
  171.6 2.0 fusion.2
  173.6 1.2 fusion.4
  174.9 2.7 fusion.5
  177.9 0.8 fusion.41
  179.3 7.1 %conditional.3 = ((f32[1,2048]{1,0:T(1,128)S(1)}, f32[1,2048]{1,0:T(1,128)S(1)}, f32[1,2048,128]{2,1,0:T(8,128)S(1)})) conditional(s32[]{:T(128)} %convert_element_type.86, (f32[1,2048]{1,0:T(1,128)S(1)}, f32[1,2048]{1,0:T(1,128)S(1)}, f32[1,2048,128]{2,1,0:T(8,128)S(1)}) %tuple.62, (pred[256,512]{0,1:T(8,128)(4,1)S(1)}, ...), branch_computations={%region_7.7_spmd, %region_8.10_spmd} | conditional | flops 551030784 | bytes 22021152 | solution.py:143
  179.8 0.6 copy.56
  180.4 2.0 fusion.2
  182.5 1.2 fusion.4
  183.7 2.7 fusion.5
  186.7 0.8 fusion.41
  188.7 7.1 %convolution_convert_fusion = bf16[256,4096]{1,0:T(8,128)(2,1)} fusion(bf16[256,1024]{0,1:T(8,128)(2,1)S(1)} %bitcast.76, bf16[1024,4096]{1,0:T(8,128)(2,1)} %param.15), kind=kOutput, calls=%fused_computation.27 | convolution fusion | flops 2148532224 | bytes 11010048 | tf_op jit(solution)/shard_map/dot_general | solution.py:175
  195.9 68.7 %reduce-scatter.2.cloned.1.call-done = bf16[256,1024]{1,0:T(8,128)(2,1)} async-done(((bf16[256,4096]{1,0:T(8,128)(2,1)}), bf16[256,1024]{1,0:T(8,128)(2,1)}) %reduce-scatter.2.cloned.1.call-update) | async-done | bytes 524304 | tf_op jit(solution)/shard_map/reduce_scatter | solution.py:176
  (139 shorter events, 11.1 us)
Async XLA Ops:
  6.5 36.5 %copy-start = (bf16[4096,128]{1,0:T(8,128)(2,1)S(1)}, bf16[4096,128]{1,0:T(8,128)(2,1)}, u32[]{:S(2)}) copy-start(bf16[4096,128]{1,0:T(8,128)(2,1)} %param.13) | copy-start | bytes 3145732
  6.5 42.8 %copy-start.3 = (s32[64]{0:T(128)S(1)}, s32[64]{0:T(128)}, u32[]{:S(2)}) copy-start(s32[64]{0:T(128)} %param.17) | copy-start | bytes 772
  6.5 36.5 %all-gather.4.cloned.1.call-start = ((), (), s32[]{:S(2)}) async-start(), calls=%async_computation.3 | async-start | bytes 2621440 | tf_op jit(solution)/shard_map/all_gather | solution.py:94
  7.3 107.0 %all-gather.6.cloned.1.call-start = ((), (), s32[]{:S(2)}) async-start(), calls=%async_computation.4 | async-start | bytes 4325376 | tf_op jit(solution)/shard_map/all_gather | solution.py:17
  43.1 7.4 %copy-start.1 = (bf16[256,4096]{1,0:T(8,128)(2,1)S(1)}, bf16[256,4096]{1,0:T(8,128)(2,1)}, u32[]{:S(2)}) copy-start(bf16[256,4096]{1,0:T(8,128)(2,1)} %all-gather.4.cloned.1.call-done) | copy-start | bytes 6291460
  58.8 19.3 %all-to-all-start = ((bf16[2,32,4096]{2,0,1:T(2,128)(2,1)}), bf16[2,32,4096]{2,0,1:T(2,128)(2,1)S(1)}, u32[]{:S(2)}, u32[]{:S(2)}) async-start(bf16[2,32,4096]{2,0,1:T(2,128)(2,1)} %copy.48), calls=%async_computation | async-start | bytes 1048576 | tf_op jit(solution)/shard_map/all_to_all | solution.py:84
  66.5 18.2 %copy-start.2 = (s32[9]{0:T(128)S(1)}, s32[9]{0:T(128)}, u32[]{:S(2)}) copy-start(s32[9]{0:T(128)} %param.16) | copy-start | bytes 112
  80.7 32.1 %all-to-all-start.1 = ((bf16[2,32,4096]{2,0,1:T(2,128)(2,1)}), bf16[2,32,4096]{2,0,1:T(2,128)(2,1)S(1)}, u32[]{:S(2)}, u32[]{:S(2)}) async-start(bf16[2,32,4096]{2,0,1:T(2,128)(2,1)} %broadcast_select_fusion), calls=%async_computation.1 | async-start | bytes 1048576 | tf_op jit(solution)/shard_map/all_to_all | solution.py:88
  84.7 179.9 %reduce-scatter.2.cloned.1.call-start = ((), (), s32[]{:S(2)}) async-start(), calls=%async_computation.5 | async-start | bytes 2621440 | tf_op jit(solution)/shard_map/reduce_scatter | solution.py:176
Sparse Core Ops, SparseCore 0:
  9.0 34.0 all-gather.3
  49.5 56.5 all-gather.5
  196.0 68.4 reduce-scatter.1
where the time goes:
time: 272 us; the launch traced here: 271 us
  waiting for transfers between devices  116 us (43%)
  matrix products  41.3 us (15%)
  other arithmetic  27.8 us (10%)
  blocking collectives  27.8 us (10%)
  local copies, waits for them, and re-layouts  23.2 us (9%)
  between operations  13.3 us (5%)
  starting transfers between devices  11.8 us (4%)
  loops' own time  9.99 us (4%)
    reduce_scatter x1, waiting for transfers between devices, output_rows(): lax.psum_scatter(head_terms.astype(jnp.bfloat16), 'tp', scatter_dimension...  68.7 us
    all_gather x1, waiting for transfers between devices, project(): portion = lax.all_gather(local_rows, 'tp', axis=1, tiled=True)  35 us
    all_gather x1, blocking collectives, attend(): lax.all_gather(key_tokens, 'cp', axis=0, tiled=True)  27.8 us
    reduce_or x16, other arithmetic, update(): jnp.any(allowed)  13.3 us
    dot_general x5, matrix products, compute(): jnp.einsum('khs,ksd->khd', weights.astype(jnp.bfloat16), per_head_values,...  13.3 us
    all_to_all x1, waiting for transfers between devices, relayout(): lax.all_to_all(pieces, 'cp', split_axis=1, concat_axis=0, tiled=True)  11.5 us
    dot_general x3, matrix products, project(): jnp.dot(portion, weight, preferred_element_type=jnp.float32)  10.9 us
    dot_general x5, matrix products, compute(): jnp.einsum('khd,ksd->khs', grouped, per_head_keys, preferred_element_type...  9.97 us
  transfers between devices with their start and end apart: 5, of which 3 were waited for; matrix products, arithmetic and copies ran while one was open for 5% of the time, Pallas kernels for 0%

commit v1 on v0

--- a/solution.py
+++ b/solution.py
@@ -91,7 +91,9 @@
 
 def project(local_rows, query_weight, key_matrix, value_matrix):
     weight_list = (query_weight, key_matrix, value_matrix)
-    portion = lax.all_gather(local_rows, "tp", axis=1, tiled=True)
+    portion = jnp.concatenate(
+        lax.all_to_all(jnp.stack([local_rows] * lax.axis_size("tp")), "tp", 0, 0), axis=1
+    )
     return tuple(
         (jnp.dot(portion, weight, preferred_element_type=jnp.float32) for weight in weight_list)
     )

time: 272 us -> 286 us (1.051)
  local copies, waits for them, and re-layouts: 23.2 us -> 44.1 us
  waiting for transfers between devices: 116 us -> 108 us
  starting transfers between devices: 11.8 us -> 18.5 us
  matrix products: 41.3 us -> 38 us
    all_gather x1 -> x0, waiting for transfers between devices: 35 us -> none  [project(): portion = lax.all_gather(local_rows, 'tp', axis=1, tiled=True)]
    all_to_all x0 -> x1, waiting for transfers between devices: none -> 25.3 us  [project(): lax.all_to_all(jnp.stack([local_rows] * lax.axis_size('tp')), 'tp', 0, 0)]
    dot_general x0 -> x1, local copies, waits for them, and re-layouts: none -> 11.3 us  [project(): jnp.dot(portion, weight, preferred_element_type=jnp.float32)]
    reshape x0 -> x3, local copies, waits for them, and re-layouts: none -> 6.42 us  [project(): jnp.concatenate(lax.all_to_all(jnp.stack([local_rows] * lax.axis_size('tp...]
    all_to_all x0 -> x1, starting transfers between devices: none -> 5.84 us  [project(): lax.all_to_all(jnp.stack([local_rows] * lax.axis_size('tp')), 'tp', 0, 0)]
    dot_general x3, matrix products: 10.9 us -> 7.44 us  [project(): jnp.dot(portion, weight, preferred_element_type=jnp.float32)]
    unnamed x11 -> x12, local copies, waits for them, and re-layouts: 6.74 us -> 6.73 us
  transfers between devices with their start and end apart: 5 -> 5, of which waited for: 3 -> 3; matrix products, arithmetic and copies ran while one was open for 5% -> 11% of each run, Pallas kernels for 0% -> 0%
where the time goes in v1:
time: 286 us; the launch traced here: 284 us
  waiting for transfers between devices  108 us (38%)
  local copies, waits for them, and re-layouts  44.1 us (15%)
  matrix products  38 us (13%)
  other arithmetic  26.4 us (9%)
  blocking collectives  26.1 us (9%)
  starting transfers between devices  18.5 us (6%)
  between operations  13.7 us (5%)
  loops' own time  9.97 us (3%)
    reduce_scatter x1, waiting for transfers between devices, output_rows(): lax.psum_scatter(head_terms.astype(jnp.bfloat16), 'tp', scatter_dimension...  68.2 us
    all_gather x1, blocking collectives, attend(): lax.all_gather(key_tokens, 'cp', axis=0, tiled=True)  26.1 us
    all_to_all x1, waiting for transfers between devices, project(): lax.all_to_all(jnp.stack([local_rows] * lax.axis_size('tp')), 'tp', 0, 0)  25.3 us
    all_to_all x1, waiting for transfers between devices, relayout(): lax.all_to_all(pieces, 'cp', split_axis=1, concat_axis=0, tiled=True)  14.3 us
    dot_general x5, matrix products, compute(): jnp.einsum('khs,ksd->khd', weights.astype(jnp.bfloat16), per_head_values,...  13.4 us
    reduce_or x16, other arithmetic, update(): jnp.any(allowed)  13.3 us
    dot_general x1, local copies, waits for them, and re-layouts, project(): jnp.dot(portion, weight, preferred_element_type=jnp.float32)  11.3 us
    dot_general x5, matrix products, compute(): jnp.einsum('khd,ksd->khs', grouped, per_head_keys, preferred_element_type...  10 us
  transfers between devices with their start and end apart: 5, of which 3 were waited for; matrix products, arithmetic and copies ran while one was open for 11% of the time, Pallas kernels for 0%

profile of v1, /device:TPU:1, one launch (start us, length us, event | category | flops | bytes accessed | tf_op | source)
XLA Modules:
  0.0 284.5 jit_solution(2724911203102471495)
XLA Ops:
  6.5 2.8 stack.2
  9.3 5.8 %all-to-all-start = ((bf16[4,256,1024]{2,1,0:T(8,128)(2,1)}), bf16[4,256,1024]{2,1,0:T(8,128)(2,1)S(1)}, u32[]{:S(2)}, u32[]{:S(2)}) async-start(bf16[4,256,1024]{2,1,0:T(8,128)(2,1)} %stack.2), calls=%async_computation | async-start | bytes 4194304 | tf_op jit(solution)/shard_map/all_to_all | solution.py:95
  15.3 25.3 %all-to-all-done = bf16[4,256,1024]{2,1,0:T(8,128)(2,1)S(1)} async-done(((bf16[4,256,1024]{2,1,0:T(8,128)(2,1)}), bf16[4,256,1024]{2,1,0:T(8,128)(2,1)S(1)}, u32[]{:S(2)}, u32[]{:S(2)}) %all-to-all-start) | async-done | bytes 2097184 | tf_op jit(solution)/shard_map/all_to_all | solution.py:95
  40.8 0.8 convolution_bitcast_fusion.1
  41.8 0.8 convolution_convert_fusion.1
  43.0 0.7 pad_maximum_fusion.1
  43.7 11.3 %copy.72 = bf16[1024,4096]{1,0:T(8,128)(2,1)} copy(bf16[1024,4096]{0,1:T(8,128)(2,1)} %bitcast.79) | data formatting | bytes 16777216 | tf_op jit(solution)/shard_map/dot_general | solution.py:98
  55.9 3.0 %copy.61 = bf16[256,4,1024]{2,1,0:T(4,128)(2,1)} copy(bf16[256,4,1024]{2,0,1:T(8,128)(2,1)S(1)} %bitcast.76) | data formatting | bytes 4194304 | tf_op jit(solution)/shard_map/reshape | solution.py:94
  58.9 3.3 %reshape.296 = bf16[256,4096,1]{1,0,2:T(8,128)(2,1)S(1)} reshape(bf16[256,4,1024]{2,1,0:T(4,128)(2,1)} %copy.61) | data formatting | bytes 4194304 | tf_op jit(solution)/shard_map/reshape | solution.py:94
  62.2 5.8 %fusion.32 = f32[256,8,128]{0,2,1:T(8,128)S(1)} fusion(bf16[256,4096,1]{1,0,2:T(8,128)(2,1)S(1)} %reshape.296, bf16[8,128,4096]{2,1,0:T(8,128)(2,1)} %bitcast.80), kind=kOutput, calls=%fused_computation.70 | convolution fusion | flops 2147483648 | bytes 11534336 | tf_op jit(solution)/shard_map/dot_general | solution.py:98
  68.7 1.3 copy.64
  70.0 8.9 %all-to-all-start.1 = ((bf16[2,32,4096]{2,0,1:T(2,128)(2,1)}), bf16[2,32,4096]{2,0,1:T(2,128)(2,1)S(1)}, u32[]{:S(2)}, u32[]{:S(2)}) async-start(bf16[2,32,4096]{2,0,1:T(2,128)(2,1)} %copy.64), calls=%async_computation.1 | async-start | bytes 1048576 | tf_op jit(solution)/shard_map/all_to_all | solution.py:84
  79.0 14.3 %all-to-all-done.1 = bf16[2,32,4096]{2,0,1:T(2,128)(2,1)S(1)} async-done(((bf16[2,32,4096]{2,0,1:T(2,128)(2,1)}), bf16[2,32,4096]{2,0,1:T(2,128)(2,1)S(1)}, u32[]{:S(2)}, u32[]{:S(2)}) %all-to-all-start.1) | async-done | bytes 524320 | tf_op jit(solution)/shard_map/all_to_all | solution.py:84
  93.4 0.9 gather_fusion
  94.3 1.5 broadcast_select_fusion
  95.8 3.7 %all-to-all-start.2 = ((bf16[2,32,4096]{2,0,1:T(2,128)(2,1)}), bf16[2,32,4096]{2,0,1:T(2,128)(2,1)S(1)}, u32[]{:S(2)}, u32[]{:S(2)}) async-start(bf16[2,32,4096]{2,0,1:T(2,128)(2,1)} %broadcast_select_fusion), calls=%async_computation.2 | async-start | bytes 1048576 | tf_op jit(solution)/shard_map/all_to_all | solution.py:88
  99.6 26.1 %all-gather = s32[32,1,256]{2,1,0:T(1,128)S(1)} all-gather(s32[1,1,256]{2,1,0:T(1,128)S(1)} %bitcast.95), channel_id=1, replica_groups=mesh['cp'=32,'tp'=4] {'cp'}, dimensions={0}, use_global_device_ids=true | all-gather | bytes 33792 | tf_op jit(solution)/shard_map/all_gather | solution.py:154
  126.5 0.9 copy.68
  127.4 3.9 %fusion.31 = (bf16[8192,128]{0,1:T(8,128)(2,1)S(1)}, bf16[8192,128]{0,1:T(8,128)(2,1)}) fusion(bf16[8192,256]{0,1:T(8,128)(2,1)} %all-gather.3.cloned.1.call-done), kind=kLoop, calls=%fused_computation.69 | loop fusion | bytes 8388608 | tf_op jit(solution)/shard_map/slice | solution.py:19
  131.3 4.1 %copy.69 = bf16[8192,128]{1,0:T(8,128)(2,1)} copy(bf16[8192,128]{0,1:T(8,128)(2,1)} %get-tuple-element.406) | data formatting | bytes 4194304
  135.4 2.4 copy.70
  137.9 63.7 %while.18 = (s32[]{:T(128)}, f32[1,2048]{1,0:T(1,128)S(1)}, f32[1,2048]{1,0:T(1,128)S(1)}, f32[1,2048,128]{2,1,0:T(8,128)S(1)}, s32[256]{0:T(256)S(1)}, /*index=...) while((s32[]{:T(128)}, f32[1,2048]{1,0:T(1,128)S(1)}, ...), condition=%wide.region_11.12_spmd.clone, body=%wide.region_4.11_spmd.clone.sunk | while | flops 551565568 | bytes 22167960 | solution.py:168
  138.3 0.8 fusion.42
  140.0 0.8 fusion.42
  141.8 0.8 fusion.42
  143.5 0.8 fusion.42
  145.2 0.8 fusion.42
  147.0 0.8 fusion.42
  148.7 0.8 fusion.42
  150.5 0.8 fusion.42
  151.9 7.2 %conditional.3 = ((f32[1,2048]{1,0:T(1,128)S(1)}, f32[1,2048]{1,0:T(1,128)S(1)}, f32[1,2048,128]{2,1,0:T(8,128)S(1)})) conditional(s32[]{:T(128)} %convert_element_type.86, (f32[1,2048]{1,0:T(1,128)S(1)}, f32[1,2048]{1,0:T(1,128)S(1)}, f32[1,2048,128]{2,1,0:T(8,128)S(1)}) %tuple.62, (pred[256,512]{0,1:T(8,128)(4,1)S(1)}, ...), branch_computations={%region_7.7_spmd, %region_8.10_spmd} | conditional | flops 551030784 | bytes 22021152 | solution.py:145
  152.4 0.6 copy.73
  153.0 2.0 fusion.2
  155.1 1.3 fusion.4
  156.4 2.7 fusion.5
  159.4 0.8 fusion.42
  160.8 7.2 %conditional.3 = ((f32[1,2048]{1,0:T(1,128)S(1)}, f32[1,2048]{1,0:T(1,128)S(1)}, f32[1,2048,128]{2,1,0:T(8,128)S(1)})) conditional(s32[]{:T(128)} %convert_element_type.86, (f32[1,2048]{1,0:T(1,128)S(1)}, f32[1,2048]{1,0:T(1,128)S(1)}, f32[1,2048,128]{2,1,0:T(8,128)S(1)}) %tuple.62, (pred[256,512]{0,1:T(8,128)(4,1)S(1)}, ...), branch_computations={%region_7.7_spmd, %region_8.10_spmd} | conditional | flops 551030784 | bytes 22021152 | solution.py:145
  161.3 0.6 copy.73
  161.9 2.0 fusion.2
  164.0 1.3 fusion.4
  165.3 2.7 fusion.5
  168.3 0.8 fusion.42
  169.7 7.2 %conditional.3 = ((f32[1,2048]{1,0:T(1,128)S(1)}, f32[1,2048]{1,0:T(1,128)S(1)}, f32[1,2048,128]{2,1,0:T(8,128)S(1)})) conditional(s32[]{:T(128)} %convert_element_type.86, (f32[1,2048]{1,0:T(1,128)S(1)}, f32[1,2048]{1,0:T(1,128)S(1)}, f32[1,2048,128]{2,1,0:T(8,128)S(1)}) %tuple.62, (pred[256,512]{0,1:T(8,128)(4,1)S(1)}, ...), branch_computations={%region_7.7_spmd, %region_8.10_spmd} | conditional | flops 551030784 | bytes 22021152 | solution.py:145
  170.2 0.6 copy.73
  170.8 2.0 fusion.2
  172.9 1.3 fusion.4
  174.2 2.7 fusion.5
  177.2 0.8 fusion.42
  179.0 0.8 fusion.42
  180.7 0.8 fusion.42
  182.5 0.8 fusion.42
  183.8 7.2 %conditional.3 = ((f32[1,2048]{1,0:T(1,128)S(1)}, f32[1,2048]{1,0:T(1,128)S(1)}, f32[1,2048,128]{2,1,0:T(8,128)S(1)})) conditional(s32[]{:T(128)} %convert_element_type.86, (f32[1,2048]{1,0:T(1,128)S(1)}, f32[1,2048]{1,0:T(1,128)S(1)}, f32[1,2048,128]{2,1,0:T(8,128)S(1)}) %tuple.62, (pred[256,512]{0,1:T(8,128)(4,1)S(1)}, ...), branch_computations={%region_7.7_spmd, %region_8.10_spmd} | conditional | flops 551030784 | bytes 22021152 | solution.py:145
  184.3 0.6 copy.73
  185.0 2.0 fusion.2
  187.0 1.3 fusion.4
  188.3 2.7 fusion.5
  191.4 0.8 fusion.42
  192.8 7.2 %conditional.3 = ((f32[1,2048]{1,0:T(1,128)S(1)}, f32[1,2048]{1,0:T(1,128)S(1)}, f32[1,2048,128]{2,1,0:T(8,128)S(1)})) conditional(s32[]{:T(128)} %convert_element_type.86, (f32[1,2048]{1,0:T(1,128)S(1)}, f32[1,2048]{1,0:T(1,128)S(1)}, f32[1,2048,128]{2,1,0:T(8,128)S(1)}) %tuple.62, (pred[256,512]{0,1:T(8,128)(4,1)S(1)}, ...), branch_computations={%region_7.7_spmd, %region_8.10_spmd} | conditional | flops 551030784 | bytes 22021152 | solution.py:145
  193.9 2.0 fusion.2
  195.9 1.3 fusion.4
  197.2 2.7 fusion.5
  200.3 0.8 fusion.42
  202.3 7.2 %convolution_convert_fusion = bf16[256,4096]{1,0:T(8,128)(2,1)} fusion(bf16[256,1024]{0,1:T(8,128)(2,1)S(1)} %bitcast.83, bf16[1024,4096]{1,0:T(8,128)(2,1)} %param.15), kind=kOutput, calls=%fused_computation.27 | convolution fusion | flops 2148532224 | bytes 11010048 | tf_op jit(solution)/shard_map/dot_general | solution.py:177
  209.5 68.2 %reduce-scatter.2.cloned.1.call-done = bf16[256,1024]{1,0:T(8,128)(2,1)} async-done(((bf16[256,4096]{1,0:T(8,128)(2,1)}), bf16[256,1024]{1,0:T(8,128)(2,1)}) %reduce-scatter.2.cloned.1.call-update) | async-done | bytes 524304 | tf_op jit(solution)/shard_map/reduce_scatter | solution.py:178
  (145 shorter events, 12.5 us)
Async XLA Ops:
  6.5 34.3 %copy-start = (bf16[4096,128]{1,0:T(8,128)(2,1)S(1)}, bf16[4096,128]{1,0:T(8,128)(2,1)}, u32[]{:S(2)}) copy-start(bf16[4096,128]{1,0:T(8,128)(2,1)} %param.13) | copy-start | bytes 3145732
  6.5 8.6 %copy-start.3 = (s32[9]{0:T(128)S(1)}, s32[9]{0:T(128)}, u32[]{:S(2)}) copy-start(s32[9]{0:T(128)} %param.16) | copy-start | bytes 112
  9.3 31.3 %all-to-all-start = ((bf16[4,256,1024]{2,1,0:T(8,128)(2,1)}), bf16[4,256,1024]{2,1,0:T(8,128)(2,1)S(1)}, u32[]{:S(2)}, u32[]{:S(2)}) async-start(bf16[4,256,1024]{2,1,0:T(8,128)(2,1)} %stack.2), calls=%async_computation | async-start | bytes 4194304 | tf_op jit(solution)/shard_map/all_to_all | solution.py:95
  15.1 112.3 %all-gather.3.cloned.1.call-start = ((), (), s32[]{:S(2)}) async-start(), calls=%async_computation.4 | async-start | bytes 4325376 | tf_op jit(solution)/shard_map/all_gather | solution.py:17
  40.6 1.2 copy-start.2
  43.7 11.3 %copy-start.4 = (s32[64]{0:T(128)S(1)}, s32[64]{0:T(128)}, u32[]{:S(2)}) copy-start(s32[64]{0:T(128)} %param.17) | copy-start | bytes 772
  70.0 23.2 %all-to-all-start.1 = ((bf16[2,32,4096]{2,0,1:T(2,128)(2,1)}), bf16[2,32,4096]{2,0,1:T(2,128)(2,1)S(1)}, u32[]{:S(2)}, u32[]{:S(2)}) async-start(bf16[2,32,4096]{2,0,1:T(2,128)(2,1)} %copy.64), calls=%async_computation.1 | async-start | bytes 1048576 | tf_op jit(solution)/shard_map/all_to_all | solution.py:84
  95.8 30.2 %all-to-all-start.2 = ((bf16[2,32,4096]{2,0,1:T(2,128)(2,1)}), bf16[2,32,4096]{2,0,1:T(2,128)(2,1)S(1)}, u32[]{:S(2)}, u32[]{:S(2)}) async-start(bf16[2,32,4096]{2,0,1:T(2,128)(2,1)} %broadcast_select_fusion), calls=%async_computation.2 | async-start | bytes 1048576 | tf_op jit(solution)/shard_map/all_to_all | solution.py:88
  99.5 178.2 %reduce-scatter.2.cloned.1.call-start = ((), (), s32[]{:S(2)}) async-start(), calls=%async_computation.5 | async-start | bytes 2621440 | tf_op jit(solution)/shard_map/reduce_scatter | solution.py:178
  202.3 75.4 %copy-start.1 = (bf16[4096,128]{1,0:T(8,128)(2,1)S(1)}, bf16[4096,128]{1,0:T(8,128)(2,1)}, u32[]{:S(2)}) copy-start(bf16[4096,128]{1,0:T(8,128)(2,1)} %param.13) | copy-start | bytes 3145732
Sparse Core Ops, SparseCore 0:
  43.8 54.7 all-gather.2
  209.6 68.0 reduce-scatter.1
